TPU v7x, 32 devices: a whole 2x2x4 slice. The times are simulated.
32 devices in a mesh: task: 4 (over y, x), tok: 8 (over z, core).
Axes of the slice: x: 2, y: 2, z: 4, core: 2. Of those that a mesh axis runs over, the one named last changes fastest.
Arguments:
- hidden: bfloat16 [4, 256, 3584], P('task', 'tok'), may hold values from -6 to 6
- attn_out: bfloat16 [4, 256, 3584], P('task', 'tok'), may hold values from -6 to 6
- gain_attn: bfloat16 [3584], replicated, may hold values from 0.5 to 1.5
- gain_mlp: bfloat16 [3584], replicated, may hold values from 0.5 to 1.5
- lengths: int32 [4, 2], P('task'), may hold values from 32 to 128
Outputs:
- gram_attn: float32 [8, 896, 1792], P('tok', 'task')
- gram_mlp: float32 [8, 896, 1792], P('tok', 'task')
All inputs are finite; a program needn't handle non-finite values.
Results may differ from a plain program's by a relative error of at most 0.0044.
Values may be sent and summed in bfloat16 or wider, within the bound.
A program may use at most 64 MiB of HBM per device.

v0:
```python
import jax
import jax.numpy as jnp
from jax import lax
from jax.sharding import PartitionSpec as P


def from_partner(block, axis, distance):
    count = lax.axis_size(axis)
    route = []
    for low in range(count):
        high = low | 1 << distance
        if high != low and high < count:
            route += [(low, high), (high, low)]
    return lax.ppermute(block, axis, route)


def normed(values, gain):
    scale = lax.rsqrt(jnp.mean(values * values, axis=-1, keepdims=True) + 1e-06)
    return values * scale * gain.astype(jnp.float32)


def per_device(hidden, attn_out, gain_attn, gain_mlp, lengths):
    tok_dev = hidden.shape[1]
    width = hidden.shape[2]
    n_tok = lax.axis_size("tok")
    n_task = lax.axis_size("task")
    block_side = min(4, max(2, n_tok // 16))
    token_parts = n_tok // (block_side * block_side)
    column_band = width // block_side
    tile_rows = column_band // token_parts
    slice_rows = tok_dev // token_parts
    seq_count = lengths.shape[1]
    seq_slots = tok_dev * n_tok // seq_count
    place = lax.axis_index("tok") * tok_dev + jnp.arange(tok_dev, dtype=jnp.int32)
    which = place // seq_slots
    offset = place % seq_slots
    owner = which[:, None] == jnp.arange(seq_count, dtype=jnp.int32)[None, :]
    limit = jnp.sum(jnp.where(owner, lengths[0][None, :], 0), axis=1)
    live = (offset < limit).astype(jnp.float32)[:, None]
    first = hidden[0].astype(jnp.float32)
    x_attn = (normed(first, gain_attn) * live).astype(jnp.bfloat16)
    mixed = first + attn_out[0].astype(jnp.float32)
    x_mlp = (normed(mixed, gain_mlp) * live).astype(jnp.bfloat16)

    def bands(values):
        split = values.reshape(token_parts, slice_rows, block_side, column_band).transpose(
            2, 0, 1, 3
        )
        shape = (block_side, block_side, token_parts, slice_rows, column_band)
        left_side = jnp.broadcast_to(split[:, None], shape).reshape(n_tok, slice_rows, column_band)
        right_side = jnp.broadcast_to(split[None], shape).reshape(n_tok, slice_rows, column_band)
        return (left_side, right_side)

    left_attn, right_attn = bands(x_attn)
    left_mlp, right_mlp = bands(x_mlp)
    arrived = (
        lax.all_to_all(left_attn, "tok", split_axis=0, concat_axis=0, tiled=True),
        lax.all_to_all(right_attn, "tok", split_axis=0, concat_axis=0, tiled=True),
        lax.all_to_all(left_mlp, "tok", split_axis=0, concat_axis=0, tiled=True),
        lax.all_to_all(right_mlp, "tok", split_axis=0, concat_axis=0, tiled=True),
    )
    contract = (((0, 1), (0, 1)), ((), ()))
    tile_attn = lax.dot_general(
        arrived[0], arrived[1], contract, preferred_element_type=jnp.float32
    )
    tile_mlp = lax.dot_general(arrived[2], arrived[3], contract, preferred_element_type=jnp.float32)
    grams = (
        tile_attn.reshape(token_parts, tile_rows, column_band),
        tile_mlp.reshape(token_parts, tile_rows, column_band),
    )
    part_index = lax.axis_index("tok") % token_parts
    depth_bits = token_parts.bit_length() - 1

    def halve(current, bit):
        upper_bit = part_index // (1 << bit) % 2 == 1
        middle = current[0].shape[0] // 2
        outgoing = tuple(
            (jnp.where(upper_bit, piece[:middle], piece[middle:]) for piece in current)
        )
        kept = tuple((jnp.where(upper_bit, piece[middle:], piece[:middle]) for piece in current))
        incoming = from_partner(outgoing, "tok", bit)
        return tuple((mine + theirs for mine, theirs in zip(kept, incoming)))

    for bit in range(depth_bits - 1, -1, -1):
        grams = halve(grams, bit)
    shaped = tuple((piece.reshape(n_task, tile_rows // n_task, column_band) for piece in grams))
    grams = lax.psum_scatter(shaped, "task", scatter_dimension=0, tiled=True)
    factor = 1.0 / (tok_dev * n_tok)
    final_attn = grams[0] * factor
    final_mlp = grams[1] * factor
    return (final_attn, final_mlp)


def solution(mesh):
    return jax.shard_map(
        per_device,
        mesh=mesh,
        in_specs=(P("task", "tok", None), P("task", "tok", None), P(), P(), P("task", None)),
        out_specs=(P("tok", "task", None), P("tok", "task", None)),
        check_vma=False,
    )
```

profile of v0, /device:TPU:0, one launch (start us, length us, event | category | flops | bytes accessed | tf_op | source)
XLA Modules:
  0.0 235.7 jit_solution(2577953144683536781)
XLA Ops:
  7.2 1.2 reshape.155
  8.4 1.3 multiply_reduce_fusion
  9.7 1.2 reshape.157
  10.9 0.7 fusion.2
  11.7 0.1 reduce_sum.31
  11.8 0.1 rsqrt.25
  11.9 0.1 rsqrt.23
  12.0 0.7 reshape.156
  12.7 0.7 reshape.158
  13.4 0.7 fusion.1
  14.2 20.1 %all_to_all.20 = bf16[8,16,1792]{2,1,0:T(8,128)(2,1)S(1)} all-to-all(bf16[8,16,1792]{2,1,0:T(8,128)(2,1)S(1)} %bitcast.31), channel_id=1, replica_groups=mesh['task'=4,'tok'=8] {'tok'}, dimensions={0} | all-to-all | bytes 917504 | tf_op jit(solution)/shard_map/all_to_all | solution.py:60
  34.2 0.8 broadcast_in_dim.27
  35.0 3.5 %all-to-all-start.2 = ((bf16[8,16,1792]{2,1,0:T(8,128)(2,1)}), bf16[8,16,1792]{2,1,0:T(8,128)(2,1)S(1)}, u32[]{:S(2)}, u32[]{:S(2)}) async-start(bf16[8,16,1792]{2,1,0:T(8,128)(2,1)} %bitcast.9), calls=%async_computation.2 | async-start | bytes 917504 | tf_op jit(solution)/shard_map/all_to_all | solution.py:59
  38.5 0.0 reduce-scatter.9.cloned.1.call-start
  38.6 13.8 %all-to-all-done.2 = bf16[8,16,1792]{2,1,0:T(8,128)(2,1)S(1)} async-done(((bf16[8,16,1792]{2,1,0:T(8,128)(2,1)}), bf16[8,16,1792]{2,1,0:T(8,128)(2,1)S(1)}, u32[]{:S(2)}, u32[]{:S(2)}) %all-to-all-start.2) | async-done | bytes 458784 | tf_op jit(solution)/shard_map/all_to_all | solution.py:59
  52.4 1.9 convolution_bitcast_fusion
  54.2 0.0 copy-start.1
  54.2 3.8 %select_bitcast_fusion = f32[1,896,1792]{2,1,0:T(8,128)} fusion(f32[1792,1792]{1,0:T(8,128)S(1)} %convolution_bitcast_fusion, pred[]{:T(512)S(6)} %eq.21), kind=kLoop, calls=%fused_computation.4 | loop fusion | flops 1605632 | bytes 19267584 | tf_op jit(solution)/shard_map/jit(_where)/select_n | solution.py:78
  58.1 2.7 %copy-done.1 = f32[1792,1792]{1,0:T(8,128)} copy-done((f32[1792,1792]{1,0:T(8,128)}, f32[1792,1792]{1,0:T(8,128)S(1)}, u32[]{:S(2)}) %copy-start.1) | copy-done | bytes 12845080
  60.8 0.0 collective-permute-start.1
  60.8 10.7 %collective-permute-done.1 = f32[1,896,1792]{2,1,0:T(8,128)} collective-permute-done((f32[1,896,1792]{2,1,0:T(8,128)}, f32[1,896,1792]{2,1,0:T(8,128)}, u32[]{:S(2)}, u32[]{:S(2)}) %collective-permute-start.1) | collective-permute-done | bytes 6422560 | tf_op jit(solution)/shard_map/ppermute | solution.py:14
  71.4 10.3 %bitcast_add_fusion = f32[1,896,1792]{2,1,0:T(8,128)} fusion(f32[1,896,1792]{2,1,0:T(8,128)} %collective-permute-done.1, f32[1792,1792]{1,0:T(8,128)} %copy-done.1, pred[]{:T(512)S(6)} %eq.21), kind=kLoop, calls=%fused_computation.2 | loop fusion | flops 3211264 | bytes 25690112 | tf_op jit(solution)/shard_map/add | solution.py:82
  81.8 0.0 reduce-scatter.9.cloned.1.call-update
  81.8 0.0 reduce-scatter.7.cloned.1.call-start
  81.9 16.3 %all_to_all.21 = bf16[8,16,1792]{2,1,0:T(8,128)(2,1)S(1)} all-to-all(bf16[8,16,1792]{2,1,0:T(8,128)(2,1)S(1)} %bitcast.32), channel_id=1, replica_groups=mesh['task'=4,'tok'=8] {'tok'}, dimensions={0} | all-to-all | bytes 917504 | tf_op jit(solution)/shard_map/all_to_all | solution.py:58
  98.3 16.3 %all_to_all.22 = bf16[8,16,1792]{2,1,0:T(8,128)(2,1)S(1)} all-to-all(bf16[8,16,1792]{2,1,0:T(8,128)(2,1)S(1)} %bitcast.30), channel_id=1, replica_groups=mesh['task'=4,'tok'=8] {'tok'}, dimensions={0} | all-to-all | bytes 917504 | tf_op jit(solution)/shard_map/all_to_all | solution.py:57
  114.6 1.9 convolution_bitcast_fusion.1
  116.5 0.0 copy-start
  116.5 3.9 %select_bitcast_fusion.1 = f32[1,896,1792]{2,1,0:T(8,128)} fusion(f32[1792,1792]{1,0:T(8,128)S(1)} %convolution_bitcast_fusion.1, pred[]{:T(512)S(6)} %eq.21), kind=kLoop, calls=%fused_computation.5 | loop fusion | flops 1605632 | bytes 19267584 | tf_op jit(solution)/shard_map/jit(_where)/select_n | solution.py:78
  120.4 2.7 %copy-done = f32[1792,1792]{1,0:T(8,128)} copy-done((f32[1792,1792]{1,0:T(8,128)}, f32[1792,1792]{1,0:T(8,128)S(1)}, u32[]{:S(2)}) %copy-start) | copy-done | bytes 12845080
  123.1 0.0 collective-permute-start
  123.1 10.7 %collective-permute-done = f32[1,896,1792]{2,1,0:T(8,128)} collective-permute-done((f32[1,896,1792]{2,1,0:T(8,128)}, f32[1,896,1792]{2,1,0:T(8,128)}, u32[]{:S(2)}, u32[]{:S(2)}) %collective-permute-start) | collective-permute-done | bytes 6422560 | tf_op jit(solution)/shard_map/ppermute | solution.py:14
  133.8 10.5 %bitcast_add_fusion.1 = f32[1,896,1792]{2,1,0:T(8,128)} fusion(f32[1,896,1792]{2,1,0:T(8,128)} %collective-permute-done, f32[1792,1792]{1,0:T(8,128)} %copy-done, pred[]{:T(512)S(6)} %eq.21), kind=kLoop, calls=%fused_computation.3 | loop fusion | flops 3211264 | bytes 25690112 | tf_op jit(solution)/shard_map/add | solution.py:82
  144.3 0.0 reduce-scatter.7.cloned.1.call-update
  144.3 7.7 %reduce-scatter.9.cloned.1.call-done = f32[1,224,1792]{2,1,0:T(8,128)} async-done(((f32[4,224,1792]{2,1,0:T(8,128)}), f32[1,224,1792]{2,1,0:T(8,128)}) %reduce-scatter.9.cloned.1.call-update) | async-done | bytes 1605648
  152.0 2.7 %broadcast_multiply_fusion = f32[1,224,1792]{2,1,0:T(8,128)} fusion(f32[1,224,1792]{2,1,0:T(8,128)} %reduce-scatter.9.cloned.1.call-done), kind=kLoop, calls=%fused_computation.6 | loop fusion | flops 401408 | bytes 3211264 | tf_op jit(solution)/shard_map/mul | solution.py:90
  154.7 71.5 %reduce-scatter.7.cloned.1.call-done = f32[1,224,1792]{2,1,0:T(8,128)} async-done(((f32[4,224,1792]{2,1,0:T(8,128)}), f32[1,224,1792]{2,1,0:T(8,128)}) %reduce-scatter.7.cloned.1.call-update) | async-done | bytes 1605648
  226.1 2.7 %broadcast_multiply_fusion.1 = f32[1,224,1792]{2,1,0:T(8,128)} fusion(f32[1,224,1792]{2,1,0:T(8,128)} %reduce-scatter.7.cloned.1.call-done), kind=kLoop, calls=%fused_computation.7 | loop fusion | flops 401408 | bytes 3211264 | tf_op jit(solution)/shard_map/mul | solution.py:89
  (8 shorter events, 0.2 us)
Async XLA Ops:
  35.0 17.3 %all-to-all-start.2 = ((bf16[8,16,1792]{2,1,0:T(8,128)(2,1)}), bf16[8,16,1792]{2,1,0:T(8,128)(2,1)S(1)}, u32[]{:S(2)}, u32[]{:S(2)}) async-start(bf16[8,16,1792]{2,1,0:T(8,128)(2,1)} %bitcast.9), calls=%async_computation.2 | async-start | bytes 917504 | tf_op jit(solution)/shard_map/all_to_all | solution.py:59
  38.5 113.5 %reduce-scatter.9.cloned.1.call-start = ((), (), s32[]{:S(2)}) async-start(), calls=%async_computation.7 | async-start | bytes 8028160
  54.2 6.5 %copy-start.1 = (f32[1792,1792]{1,0:T(8,128)}, f32[1792,1792]{1,0:T(8,128)S(1)}, u32[]{:S(2)}) copy-start(f32[1792,1792]{1,0:T(8,128)S(1)} %convolution_bitcast_fusion) | copy-start | bytes 38535172
  60.8 10.7 %collective-permute-start.1 = (f32[1,896,1792]{2,1,0:T(8,128)}, f32[1,896,1792]{2,1,0:T(8,128)}, u32[]{:S(2)}, u32[]{:S(2)}) collective-permute-start(f32[1,896,1792]{2,1,0:T(8,128)} %select_bitcast_fusion), channel_id=1, source_target_pairs={{0,1},{1,0},{2,3},{3,2},{4,5},{5,4},{6,7},{7,6},{8,9},{9,8},{10,11... | collective-permute-start | bytes 19267592 | tf_op jit(solution)/shard_map/ppermute | solution.py:14
  81.8 144.3 %reduce-scatter.7.cloned.1.call-start = ((), (), s32[]{:S(2)}) async-start(), calls=%async_computation.6 | async-start | bytes 8028160
  116.5 6.6 %copy-start = (f32[1792,1792]{1,0:T(8,128)}, f32[1792,1792]{1,0:T(8,128)S(1)}, u32[]{:S(2)}) copy-start(f32[1792,1792]{1,0:T(8,128)S(1)} %convolution_bitcast_fusion.1) | copy-start | bytes 38535172
  123.1 10.7 %collective-permute-start = (f32[1,896,1792]{2,1,0:T(8,128)}, f32[1,896,1792]{2,1,0:T(8,128)}, u32[]{:S(2)}, u32[]{:S(2)}) collective-permute-start(f32[1,896,1792]{2,1,0:T(8,128)} %select_bitcast_fusion.1), channel_id=1, source_target_pairs={{0,1},{1,0},{2,3},{3,2},{4,5},{5,4},{6,7},{7,6},{8,9},{9,8},{10,11... | collective-permute-start | bytes 19267592 | tf_op jit(solution)/shard_map/ppermute | solution.py:14
Sparse Core Ops, SparseCore 0:
  81.9 70.0 reduce-scatter.8
  155.0 71.1 reduce-scatter.6
where the time goes:
time: 236 us
  waiting for transfers between devices  114 us (48%)
  blocking collectives  52.7 us (22%)
  other arithmetic  36.7 us (16%)
  between operations  14.2 us (6%)
  local copies, waits for them, and re-layouts  10.5 us (4%)
  matrix products  3.72 us (2%)
  starting transfers between devices  3.56 us (2%)
    unnamed x4, waiting for transfers between devices  79.2 us
    ppermute x2, waiting for transfers between devices, from_partner(): return lax.ppermute(block, axis, route)  21.4 us
    add x2, other arithmetic, halve(): return tuple((mine + theirs for mine, theirs in zip(kept, incoming)))  20.8 us
    all_to_all x1, blocking collectives, per_device(): lax.all_to_all(right_mlp, 'tok', split_axis=0, concat_axis=0, tiled=True)  20.1 us
    all_to_all x1, blocking collectives, per_device(): lax.all_to_all(left_attn, 'tok', split_axis=0, concat_axis=0, tiled=True)  16.3 us
    all_to_all x1, blocking collectives, per_device(): lax.all_to_all(right_attn, 'tok', split_axis=0, concat_axis=0, tiled=True)  16.3 us
    all_to_all x1, waiting for transfers between devices, per_device(): lax.all_to_all(left_mlp, 'tok', split_axis=0, concat_axis=0, tiled=True)  13.8 us
    select_n x2, other arithmetic, halve(): jnp.where(upper_bit, piece[:middle], piece[middle:])  7.74 us
  transfers between devices with their start and end apart: 5, of which 5 were waited for; matrix products, arithmetic and copies ran while one was open for 8% of the time, Pallas kernels for 0%

commit v1 on v0

--- a/solution.py
+++ b/solution.py
@@ -1,7 +1,296 @@
+import functools
+
 import jax
 import jax.numpy as jnp
 from jax import lax
+from jax.experimental import pallas as pl
+from jax.experimental.pallas import tpu as pltpu
 from jax.sharding import PartitionSpec as P
+
+LANES = 128
+
+
+def gather_kernel(
+    hidden, attn_out, gain_attn, gain_mlp, lengths, out_attn, out_mlp,
+    mine, held, rows, total, got, row_got, row_sent, z_sent, side_sent, pair_sent,
+):
+    task, tok = lax.axis_index("task"), lax.axis_index("tok")
+    n_task = lax.axis_size("task")
+    plane, core = tok // 2, tok % 2
+    band = plane % 2
+    tok_dev, column_band = held.shape[2], held.shape[3]
+    n_planes = held.shape[1] // (2 * n_task)
+    inner = jnp.logical_or(plane == 1, plane == 2)
+    outer = jnp.logical_not(inner)
+
+    def flip(value, bit):
+        return value + bit - 2 * bit * (value // bit % 2)
+
+    task_x, task_y = flip(task, 1), flip(task, 2)
+    task_d = flip(task_x, 2)
+    plane_1, plane_2 = flip(plane, 1), flip(plane, 2)
+    plane_3 = flip(plane_1, 2)
+    near, far = jnp.where(inner, plane_3, plane_2), jnp.where(inner, plane_2, plane_3)
+    order = (plane, plane_1, near, far)
+
+    def at(tasks, planes, cores):
+        return {"task": tasks, "tok": planes * 2 + cores}
+
+    def chunk(planes, tasks, cores):
+        return planes * (2 * n_task) + tasks * 2 + cores
+
+    own = chunk(plane, task, core)
+
+    slab = 16
+    seq_count = lengths.shape[1]
+    seq_slots = tok_dev * lax.axis_size("tok") // seq_count
+    for low in range(0, tok_dev, slab):
+        part = pl.ds(low, slab)
+        place = tok * tok_dev + low + lax.broadcasted_iota(jnp.int32, (slab, 1), 0)
+        live = jnp.zeros((slab, 1), jnp.float32)
+        for seq in range(seq_count):
+            offset = place - seq * seq_slots
+            inside = (offset >= 0) & (offset < seq_slots) & (offset < lengths[0, seq])
+            live = jnp.where(inside, 1.0, live)
+        first = hidden[0, part, :].astype(jnp.float32)
+        mixed = first + attn_out[0, part, :].astype(jnp.float32)
+        for which, values, gain in ((0, first, gain_attn), (1, mixed, gain_mlp)):
+            done = (normed(values, gain[...]) * live).astype(jnp.bfloat16)
+            for side in range(2):
+                mine[which, side, part, :] = done[:, side * column_band : (side + 1) * column_band]
+    for which in range(2):
+        held[which, own] = mine[which, band]
+
+    peers = (
+        at(task_x, plane, core), at(task_y, plane, core), at(task, plane, 1 - core),
+        at(task, plane_1, core), at(task, plane_2, core), at(task, plane_3, core),
+    )
+    barrier = pltpu.get_barrier_semaphore()
+    for peer in peers:
+        pl.semaphore_signal(
+            barrier, inc=1, device_id=peer, device_id_type=pl.DeviceIdType.MESH
+        )
+    pl.semaphore_wait(barrier, len(peers))
+    to_x, to_y, to_pair, to_1, to_2, to_3 = peers
+
+    def copy(source, which, q, sent, peer):
+        return pltpu.make_async_remote_copy(
+            src_ref=source, dst_ref=held.at[which, q], send_sem=sent,
+            recv_sem=got.at[which, q], device_id=peer,
+            device_id_type=pl.DeviceIdType.MESH,
+        )
+
+    started = []
+
+    def send(*arguments):
+        out = copy(*arguments)
+        out.start()
+        started.append(out)
+
+    def arrive(which, q):
+        copy(held.at[which, q], which, q, pair_sent.at[which, q], to_pair).wait_recv()
+
+    def to_inner(which):
+        return copy(mine.at[which, 1 - band], which, own, z_sent.at[which, 2], to_3)
+
+    def relay(which):
+        q = chunk(plane_1, task, core)
+        return copy(held.at[which, q], which, q, z_sent.at[which, 3], to_2)
+
+    def own_step(step):
+        for which in range(2):
+            q = chunk(order[step], task, core)
+            if step:
+                arrive(which, q)
+                source = held.at[which, q]
+            else:
+                source = mine.at[which, band]
+            if step == 1:
+                @pl.when(inner)
+                def _():
+                    relay(which).start()
+            send(source, which, q, side_sent.at[0, which, step], to_x)
+            send(source, which, q, side_sent.at[1, which, step], to_y)
+            if step == 0:
+                @pl.when(inner)
+                def _():
+                    to_inner(which).start()
+                send(mine.at[which, 1 - band], which, own, z_sent.at[which, 0], to_1)
+                send(source, which, own, z_sent.at[which, 1], to_2)
+            send(source, which, q, pair_sent.at[which, q], to_pair)
+
+    def side_step(step):
+        for which in range(2):
+            for tasks, relayed, axis, peer in (
+                (task_x, 0, 1, to_y), (task_y, 1, 0, to_x)
+            ):
+                q = chunk(order[step], tasks, core)
+                arrive(which, q)
+                if which == relayed:
+                    send(
+                        held.at[which, q], which, q,
+                        side_sent.at[axis, which, n_planes + step], peer,
+                    )
+                send(held.at[which, q], which, q, pair_sent.at[which, q], to_pair)
+
+    def diagonal_step(step):
+        for which in range(2):
+            q = chunk(order[step], task_d, core)
+            arrive(which, q)
+            send(held.at[which, q], which, q, pair_sent.at[which, q], to_pair)
+
+    row_count = out_attn.shape[1]
+    padded = rows.shape[3]
+    window = min(padded + LANES, column_band)
+    row_start = core * (column_band // 2) + task * row_count
+    base = jnp.minimum(row_start // LANES * LANES, column_band - window)
+    shift = window - (row_start - base)
+
+    def row_copy(group):
+        return pltpu.make_async_remote_copy(
+            src_ref=rows.at[group], dst_ref=rows.at[group], send_sem=row_sent.at[group],
+            recv_sem=row_got.at[group], device_id=to_1,
+            device_id_type=pl.DeviceIdType.MESH,
+        )
+
+    def rows_of(step, tasks, other_arrived=True):
+        for which in range(2):
+            arrive(which, chunk(order[step], tasks, 1 - core))
+        group = order[step] * n_task + tasks
+
+        @pl.when(outer)
+        def _():
+            for which in range(2):
+                span = held[
+                    which, pl.ds(group * 2, 2), :, pl.ds(pl.multiple_of(base, LANES), window)
+                ]
+                span = span.reshape(2 * tok_dev, window).astype(jnp.float32)
+                span = pltpu.roll(span, shift, 1)
+                rows[group, which] = span[:, :padded].astype(jnp.bfloat16)
+
+        return group
+
+    def send_rows(group):
+        @pl.when(outer)
+        def _():
+            row_copy(group).start()
+
+    def cut(step, members):
+        waiting = None
+        for tasks in members:
+            group = rows_of(step, tasks)
+            if waiting is not None:
+                send_rows(waiting)
+            waiting = group
+        return waiting
+
+    def product(step, which):
+        left = rows[pl.ds(order[step] * n_task, n_task), which]
+        right = held[which, pl.ds(order[step] * 2 * n_task, 2 * n_task)]
+        depth = 2 * n_task * tok_dev
+        return lax.dot_general(
+            left.reshape(depth, padded), right.reshape(depth, column_band),
+            (((0,), (0,)), ((), ())), preferred_element_type=jnp.float32,
+        )
+
+    def rows_arrive(step):
+        @pl.when(inner)
+        def _():
+            for tasks in range(n_task):
+                row_copy(order[step] * n_task + tasks).wait_recv()
+
+    def multiply(step):
+        rows_arrive(step)
+
+        @pl.loop(0, 2)
+        def _(which):
+            piece = product(step, which)
+            if step == 0:
+                total[which] = piece
+            else:
+                total[which] += piece
+
+    sides = (task, task_x, task_y)
+    own_step(0)
+    own_step(1)
+    side_step(0)
+    own_step(2)
+    side_step(1)
+    diagonal_step(0)
+    waiting = cut(0, sides + (task_d,))
+    own_step(3)
+    send_rows(waiting)
+    side_step(2)
+    diagonal_step(1)
+    waiting = cut(1, sides + (task_d,))
+    multiply(0)
+    send_rows(waiting)
+    waiting = cut(2, sides)
+    side_step(3)
+    send_rows(waiting)
+    diagonal_step(2)
+    waiting = cut(2, (task_d,))
+    multiply(1)
+    send_rows(waiting)
+    waiting = cut(3, sides)
+    diagonal_step(3)
+    send_rows(waiting)
+    waiting = cut(3, (task_d,))
+    multiply(2)
+    send_rows(waiting)
+    rows_arrive(3)
+    factor = 1.0 / (tok_dev * lax.axis_size("tok"))
+    for which, out in ((0, out_attn), (1, out_mlp)):
+        piece = total[which] + product(3, which)
+        out[0] = piece[:row_count] * factor
+
+    for out in started:
+        out.wait_send()
+
+    @pl.when(inner)
+    def _():
+        for which in range(2):
+            to_inner(which).wait_send()
+            relay(which).wait_send()
+
+    @pl.when(outer)
+    def _():
+        for group in range(n_planes * n_task):
+            row_copy(group).wait_send()
+
+
+def gathered(hidden, attn_out, gain_attn, gain_mlp, lengths):
+    _, tok_dev, width = hidden.shape
+    n_tok, n_task = lax.axis_size("tok"), lax.axis_size("task")
+    column_band = width // 2
+    row_count = column_band // 2 // n_task
+    padded = -(-row_count // LANES) * LANES
+    devices = n_tok * n_task
+    groups = devices // 2
+    vmem = pl.BlockSpec(memory_space=pltpu.VMEM)
+    shape = jax.ShapeDtypeStruct((1, row_count, column_band), jnp.float32)
+    semaphores = pltpu.SemaphoreType.DMA
+    return pl.pallas_call(
+        gather_kernel,
+        out_shape=(shape, shape),
+        in_specs=[vmem] * 4 + [pl.BlockSpec(memory_space=pltpu.SMEM)],
+        out_specs=(vmem, vmem),
+        scratch_shapes=[
+            pltpu.VMEM((2, 2, tok_dev, column_band), jnp.bfloat16),
+            pltpu.VMEM((2, devices, tok_dev, column_band), jnp.bfloat16),
+            pltpu.VMEM((groups, 2, 2 * tok_dev, padded), jnp.bfloat16),
+            pltpu.VMEM((2, padded, column_band), jnp.float32),
+            semaphores((2, devices)),
+            semaphores((groups,)),
+            semaphores((groups,)),
+            semaphores((2, 4)),
+            semaphores((2, 2, n_tok)),
+            semaphores((2, devices)),
+        ],
+        compiler_params=pltpu.CompilerParams(
+            collective_id=0, has_side_effects=True, vmem_limit_bytes=48 * 2**20
+        ),
+    )(hidden, attn_out, gain_attn.reshape(1, width), gain_mlp.reshape(1, width), lengths)
 
 
 def from_partner(block, axis, distance):
@@ -26,6 +315,8 @@
     n_task = lax.axis_size("task")
     block_side = min(4, max(2, n_tok // 16))
     token_parts = n_tok // (block_side * block_side)
+    if (n_task, n_tok, block_side) == (4, 8, 2) and width % (4 * LANES) == 0 and tok_dev % 16 == 0:
+        return gathered(hidden, attn_out, gain_attn, gain_mlp, lengths)
     column_band = width // block_side
     tile_rows = column_band // token_parts
     slice_rows = tok_dev // token_parts

time: 236 us -> 55 us (0.23)
  waiting for transfers between devices: 114 us -> 0 us
  blocking collectives: 52.7 us -> 0 us
  Pallas kernels: 0 us -> 47.1 us
  other arithmetic: 36.7 us -> 0 us
  between operations: 14.2 us -> 0.65 us
  local copies, waits for them, and re-layouts: 10.5 us -> 6.25 us
  matrix products: 3.72 us -> 0 us
  starting transfers between devices: 3.56 us -> 0 us
    unnamed x4 -> x0, waiting for transfers between devices: 79.2 us -> none
    all_to_all x3 -> x0, blocking collectives: 52.7 us -> none  [the longest x1 20.1 us: per_device(): lax.all_to_all(right_mlp, 'tok', split_axis=0, concat_axis=0, tiled=True)]
    pallas_call x0 -> x1, Pallas kernels: none -> 47.1 us  [gathered(): pl.pallas_call(gather_kernel, out_shape=(shape, shape), in_specs=[vmem] *...]
    ppermute x2 -> x0, waiting for transfers between devices: 21.4 us -> none  [from_partner(): return lax.ppermute(block, axis, route)]
    add x2 -> x0, other arithmetic: 20.8 us -> none  [halve(): return tuple((mine + theirs for mine, theirs in zip(kept, incoming)))]
    all_to_all x1 -> x0, waiting for transfers between devices: 13.8 us -> none  [per_device(): lax.all_to_all(left_mlp, 'tok', split_axis=0, concat_axis=0, tiled=True)]
    select_n x3 -> x0, other arithmetic: 7.75 us -> none  [the longest x2 7.74 us: halve(): jnp.where(upper_bit, piece[:middle], piece[middle:])]
    mul x2 -> x0, other arithmetic: 5.35 us -> none  [the longest x1 2.68 us: per_device(): final_mlp = grams[1] * factor]
  transfers between devices with their start and end apart: 5 -> 0, of which waited for: 5 -> 0; matrix products, arithmetic and copies ran while one was open for 8% -> 0% of each run, Pallas kernels for 0% -> 0%
where the time goes in v1:
time: 55 us; the launch traced here: 54 us
  Pallas kernels  47.1 us (86%)
  local copies, waits for them, and re-layouts  6.25 us (11%)
  between operations  0.65 us (1%)
    pallas_call x1, Pallas kernels, gathered(): pl.pallas_call(gather_kernel, out_shape=(shape, shape), in_specs=[vmem] *...  47.1 us
    unnamed x8, local copies, waits for them, and re-layouts  4.83 us

profile of v1, /device:TPU:0, one launch (start us, length us, event | category | flops | bytes accessed | tf_op | source)
XLA Modules:
  0.0 54.0 jit_solution(11431008009931499896)
XLA Ops:
  0.6 0.7 %reshape.10.gain_attn = bf16[1,3584]{1,0:T(2,128)(2,1)S(1)} reshape(bf16[3584]{0:T(1024)(128)(2,1)} %param.7) | data formatting | bytes 14336 | tf_op jit(solution)/shard_map/reshape | solution.py:293
  1.3 0.7 %reshape.11.gain_mlp = bf16[1,3584]{1,0:T(2,128)(2,1)S(1)} reshape(bf16[3584]{0:T(1024)(128)(2,1)} %param.8) | data formatting | bytes 14336 | tf_op jit(solution)/shard_map/reshape | solution.py:293
  2.1 0.0 copy-start
  2.1 0.9 %copy-done = bf16[1,32,3584]{2,1,0:T(8,128)(2,1)S(1)} copy-done((bf16[1,32,3584]{2,1,0:T(8,128)(2,1)S(1)}, bf16[1,32,3584]{2,1,0:T(8,128)(2,1)}, u32[]{:S(2)}) %copy-start) | copy-done | bytes 229400
  3.0 0.0 copy-start.1
  3.0 0.9 %copy-done.1 = bf16[1,32,3584]{2,1,0:T(8,128)(2,1)S(1)} copy-done((bf16[1,32,3584]{2,1,0:T(8,128)(2,1)S(1)}, bf16[1,32,3584]{2,1,0:T(8,128)(2,1)}, u32[]{:S(2)}) %copy-start.1) | copy-done | bytes 229400
  3.9 0.0 copy-start.2
  3.9 0.7 %copy-done.2 = s32[1,2]{1,0:T(1,128)S(1)} copy-done((s32[1,2]{1,0:T(1,128)S(1)}, s32[1,2]{1,0:T(1,128)}, u32[]{:S(2)}) %copy-start.2) | copy-done | bytes 32
  4.6 47.1 %shard_map.68 = (f32[1,224,1792]{2,1,0:T(8,128)S(1)}, f32[1,224,1792]{2,1,0:T(8,128)S(1)}) custom-call(bf16[1,32,3584]{2,1,0:T(8,128)(2,1)S(1)} %copy-done, bf16[1,32,3584]{2,1,0:T(8,128)(2,1)S(1)} %copy-done.1, bf16[1,3584]{1,0:T(2,128)(2,1)S(1)} %reshape.10.gain_attn, bf16[1,3584]{1,0:T(2,128)(2,1)S(1)} %reshape.11.gain_mlp, s32[1,2]{1,0:T(1,128)S(1)} %copy-done.2), custom_call_target="tpu_custom_call" | custom-call | tf_op jit(solution)/shard_map/pallas_call | solution.py:273
  51.7 1.2 %copy.9 = f32[1,224,1792]{2,1,0:T(8,128)} copy(f32[1,224,1792]{2,1,0:T(8,128)S(1)} %get-tuple-element.4) | data formatting | bytes 3211264
  52.8 1.2 %copy.10 = f32[1,224,1792]{2,1,0:T(8,128)} copy(f32[1,224,1792]{2,1,0:T(8,128)S(1)} %get-tuple-element.5) | data formatting | bytes 3211264
Async XLA Ops:
  2.1 0.9 %copy-start = (bf16[1,32,3584]{2,1,0:T(8,128)(2,1)S(1)}, bf16[1,32,3584]{2,1,0:T(8,128)(2,1)}, u32[]{:S(2)}) copy-start(bf16[1,32,3584]{2,1,0:T(8,128)(2,1)} %hidden.1) | copy-start | bytes 688132
  3.0 0.9 %copy-start.1 = (bf16[1,32,3584]{2,1,0:T(8,128)(2,1)S(1)}, bf16[1,32,3584]{2,1,0:T(8,128)(2,1)}, u32[]{:S(2)}) copy-start(bf16[1,32,3584]{2,1,0:T(8,128)(2,1)} %attn_out.1) | copy-start | bytes 688132
  3.9 0.7 %copy-start.2 = (s32[1,2]{1,0:T(1,128)S(1)}, s32[1,2]{1,0:T(1,128)}, u32[]{:S(2)}) copy-start(s32[1,2]{1,0:T(1,128)} %lengths.1) | copy-start | bytes 28

commit v2 on v1

--- a/solution.py
+++ b/solution.py
@@ -10,9 +10,54 @@
 LANES = 128
 
 
+def planes_in_product_order():
+    plane = lax.axis_index("tok") // 2
+    inner = jnp.logical_or(plane == 1, plane == 2)
+    plane_1 = plane + 1 - 2 * (plane % 2)
+    plane_2 = jnp.where(plane // 2 == 1, plane - 2, plane + 2)
+    plane_3 = 3 - plane
+    return (
+        jnp.where(inner, plane_1, plane), jnp.where(inner, plane, plane_1),
+        jnp.where(inner, plane_3, plane_2), jnp.where(inner, plane_2, plane_3),
+    )
+
+
+def product(rows, held, plane, which, columns=slice(None)):
+    n_task = lax.axis_size("task")
+    left = rows[pl.ds(plane * n_task, n_task), which]
+    right = held[which, pl.ds(plane * 2 * n_task, 2 * n_task), :, columns]
+    depth = left.shape[0] * left.shape[1]
+    return lax.dot_general(
+        left.reshape(depth, left.shape[2]), right.reshape(depth, right.shape[2]),
+        (((0,), (0,)), ((), ())), preferred_element_type=jnp.float32,
+    )
+
+
+def last_kernel(held, rows, total, out_attn, out_mlp, staged, sent):
+    row_count, column_band = out_attn.shape[1], out_attn.shape[2]
+    plane = planes_in_product_order()[3]
+    factor = 1.0 / (lax.axis_size("tok") * held.shape[2])
+    n_bands = sent.shape[1]
+    width = column_band // n_bands
+    writes = []
+    for which, out in ((0, out_attn), (1, out_mlp)):
+        for band in range(n_bands):
+            span = slice(band * width, (band + 1) * width)
+            piece = total[which, :, span] + product(rows, held, plane, which, span)
+            staged[which, 0, :, span] = piece[:row_count] * factor
+            write = pltpu.make_async_copy(
+                staged.at[which, :, :, span], out.at[:, :, span], sent.at[which, band]
+            )
+            write.start()
+            writes.append(write)
+    for write in writes:
+        write.wait()
+
+
 def gather_kernel(
-    hidden, attn_out, gain_attn, gain_mlp, lengths, out_attn, out_mlp,
-    mine, held, rows, total, got, row_got, row_sent, z_sent, side_sent, pair_sent,
+    hidden_hbm, attn_hbm, gain_attn_hbm, gain_mlp_hbm, lengths_hbm, held, rows, total,
+    hidden, attn_out, gain_attn, gain_mlp, lengths, mine,
+    loaded, got, row_got, row_sent, z_sent, side_sent, pair_sent,
 ):
     task, tok = lax.axis_index("task"), lax.axis_index("tok")
     n_task = lax.axis_size("task")
@@ -32,6 +77,7 @@
     plane_3 = flip(plane_1, 2)
     near, far = jnp.where(inner, plane_3, plane_2), jnp.where(inner, plane_2, plane_3)
     order = (plane, plane_1, near, far)
+    product_order = planes_in_product_order()
 
     def at(tasks, planes, cores):
         return {"task": tasks, "tok": planes * 2 + cores}
@@ -40,6 +86,27 @@
         return planes * (2 * n_task) + tasks * 2 + cores
 
     own = chunk(plane, task, core)
+
+    loads = [
+        pltpu.make_async_copy(source, target, loaded.at[spot])
+        for spot, (source, target) in enumerate((
+            (hidden_hbm, hidden), (attn_hbm, attn_out), (gain_attn_hbm, gain_attn),
+            (gain_mlp_hbm, gain_mlp), (lengths_hbm, lengths),
+        ))
+    ]
+    for load in loads:
+        load.start()
+    peers = (
+        at(task_x, plane, core), at(task_y, plane, core), at(task, plane, 1 - core),
+        at(task, plane_1, core), at(task, plane_2, core), at(task, plane_3, core),
+    )
+    barrier = pltpu.get_barrier_semaphore()
+    for peer in peers:
+        pl.semaphore_signal(
+            barrier, inc=1, device_id=peer, device_id_type=pl.DeviceIdType.MESH
+        )
+    for load in loads:
+        load.wait()
 
     slab = 16
     seq_count = lengths.shape[1]
@@ -55,21 +122,12 @@
         first = hidden[0, part, :].astype(jnp.float32)
         mixed = first + attn_out[0, part, :].astype(jnp.float32)
         for which, values, gain in ((0, first, gain_attn), (1, mixed, gain_mlp)):
-            done = (normed(values, gain[...]) * live).astype(jnp.bfloat16)
+            done = (normed(values, gain[...].reshape(1, -1)) * live).astype(jnp.bfloat16)
             for side in range(2):
                 mine[which, side, part, :] = done[:, side * column_band : (side + 1) * column_band]
     for which in range(2):
         held[which, own] = mine[which, band]
 
-    peers = (
-        at(task_x, plane, core), at(task_y, plane, core), at(task, plane, 1 - core),
-        at(task, plane_1, core), at(task, plane_2, core), at(task, plane_3, core),
-    )
-    barrier = pltpu.get_barrier_semaphore()
-    for peer in peers:
-        pl.semaphore_signal(
-            barrier, inc=1, device_id=peer, device_id_type=pl.DeviceIdType.MESH
-        )
     pl.semaphore_wait(barrier, len(peers))
     to_x, to_y, to_pair, to_1, to_2, to_3 = peers
 
@@ -97,49 +155,46 @@
         q = chunk(plane_1, task, core)
         return copy(held.at[which, q], which, q, z_sent.at[which, 3], to_2)
 
-    def own_step(step):
-        for which in range(2):
-            q = chunk(order[step], task, core)
-            if step:
-                arrive(which, q)
-                source = held.at[which, q]
-            else:
-                source = mine.at[which, band]
-            if step == 1:
-                @pl.when(inner)
-                def _():
-                    relay(which).start()
-            send(source, which, q, side_sent.at[0, which, step], to_x)
-            send(source, which, q, side_sent.at[1, which, step], to_y)
-            if step == 0:
-                @pl.when(inner)
-                def _():
-                    to_inner(which).start()
-                send(mine.at[which, 1 - band], which, own, z_sent.at[which, 0], to_1)
-                send(source, which, own, z_sent.at[which, 1], to_2)
-            send(source, which, q, pair_sent.at[which, q], to_pair)
-
-    def side_step(step):
-        for which in range(2):
-            for tasks, relayed, axis, peer in (
-                (task_x, 0, 1, to_y), (task_y, 1, 0, to_x)
-            ):
-                q = chunk(order[step], tasks, core)
-                arrive(which, q)
-                if which == relayed:
-                    send(
-                        held.at[which, q], which, q,
-                        side_sent.at[axis, which, n_planes + step], peer,
-                    )
-                send(held.at[which, q], which, q, pair_sent.at[which, q], to_pair)
-
-    def diagonal_step(step):
-        for which in range(2):
-            q = chunk(order[step], task_d, core)
+    def own_step(step, which):
+        q = chunk(order[step], task, core)
+        if step:
             arrive(which, q)
+            source = held.at[which, q]
+        else:
+            source = mine.at[which, band]
+        if step == 1:
+            @pl.when(inner)
+            def _():
+                relay(which).start()
+        send(source, which, q, side_sent.at[0, which, step], to_x)
+        send(source, which, q, side_sent.at[1, which, step], to_y)
+        if step == 0:
+            @pl.when(inner)
+            def _():
+                to_inner(which).start()
+            send(mine.at[which, 1 - band], which, own, z_sent.at[which, 0], to_1)
+            send(source, which, own, z_sent.at[which, 1], to_2)
+        send(source, which, q, pair_sent.at[which, q], to_pair)
+
+    def side_step(step, which):
+        for tasks, relayed, axis, peer in (
+            (task_x, 0, 1, to_y), (task_y, 1, 0, to_x)
+        ):
+            q = chunk(order[step], tasks, core)
+            arrive(which, q)
+            if which == relayed:
+                send(
+                    held.at[which, q], which, q,
+                    side_sent.at[axis, which, n_planes + step], peer,
+                )
             send(held.at[which, q], which, q, pair_sent.at[which, q], to_pair)
 
-    row_count = out_attn.shape[1]
+    def diagonal_step(step, which):
+        q = chunk(order[step], task_d, core)
+        arrive(which, q)
+        send(held.at[which, q], which, q, pair_sent.at[which, q], to_pair)
+
+    row_count = column_band // 2 // n_task
     padded = rows.shape[3]
     window = min(padded + LANES, column_band)
     row_start = core * (column_band // 2) + task * row_count
@@ -184,65 +239,59 @@
             waiting = group
         return waiting
 
-    def product(step, which):
-        left = rows[pl.ds(order[step] * n_task, n_task), which]
-        right = held[which, pl.ds(order[step] * 2 * n_task, 2 * n_task)]
-        depth = 2 * n_task * tok_dev
-        return lax.dot_general(
-            left.reshape(depth, padded), right.reshape(depth, column_band),
-            (((0,), (0,)), ((), ())), preferred_element_type=jnp.float32,
-        )
-
     def rows_arrive(step):
         @pl.when(inner)
         def _():
             for tasks in range(n_task):
-                row_copy(order[step] * n_task + tasks).wait_recv()
+                row_copy(product_order[step] * n_task + tasks).wait_recv()
 
     def multiply(step):
         rows_arrive(step)
 
         @pl.loop(0, 2)
         def _(which):
-            piece = product(step, which)
+            piece = product(rows, held, product_order[step], which)
             if step == 0:
                 total[which] = piece
             else:
                 total[which] += piece
 
     sides = (task, task_x, task_y)
-    own_step(0)
-    own_step(1)
-    side_step(0)
-    own_step(2)
-    side_step(1)
-    diagonal_step(0)
-    waiting = cut(0, sides + (task_d,))
-    own_step(3)
-    send_rows(waiting)
-    side_step(2)
-    diagonal_step(1)
-    waiting = cut(1, sides + (task_d,))
+    everyone = sides + (task_d,)
+    for which in range(2):
+        own_step(0, which)
+    for which in range(2):
+        own_step(1, which)
+        side_step(0, which)
+    for which in range(2):
+        own_step(2, which)
+        side_step(1, which)
+        diagonal_step(0, which)
+    waiting = cut(0, everyone)
+    for which in range(2):
+        own_step(3, which)
+        if which == 0:
+            send_rows(waiting)
+        side_step(2, which)
+        diagonal_step(1, which)
+    waiting = cut(1, everyone)
+    for which in range(2):
+        side_step(3, which)
+        if which == 0:
+            send_rows(waiting)
+        diagonal_step(2, which)
+    waiting = cut(2, everyone)
     multiply(0)
     send_rows(waiting)
-    waiting = cut(2, sides)
-    side_step(3)
-    send_rows(waiting)
-    diagonal_step(2)
-    waiting = cut(2, (task_d,))
+    waiting = cut(3, sides)
     multiply(1)
     send_rows(waiting)
-    waiting = cut(3, sides)
-    diagonal_step(3)
-    send_rows(waiting)
+    for which in range(2):
+        diagonal_step(3, which)
     waiting = cut(3, (task_d,))
     multiply(2)
     send_rows(waiting)
     rows_arrive(3)
-    factor = 1.0 / (tok_dev * lax.axis_size("tok"))
-    for which, out in ((0, out_attn), (1, out_mlp)):
-        piece = total[which] + product(3, which)
-        out[0] = piece[:row_count] * factor
 
     for out in started:
         out.wait_send()
@@ -267,19 +316,25 @@
     padded = -(-row_count // LANES) * LANES
     devices = n_tok * n_task
     groups = devices // 2
-    vmem = pl.BlockSpec(memory_space=pltpu.VMEM)
-    shape = jax.ShapeDtypeStruct((1, row_count, column_band), jnp.float32)
+    vmem, hbm = (pl.BlockSpec(memory_space=space) for space in (pltpu.VMEM, pltpu.HBM))
     semaphores = pltpu.SemaphoreType.DMA
-    return pl.pallas_call(
+    held, rows, total = pl.pallas_call(
         gather_kernel,
-        out_shape=(shape, shape),
-        in_specs=[vmem] * 4 + [pl.BlockSpec(memory_space=pltpu.SMEM)],
-        out_specs=(vmem, vmem),
+        out_shape=(
+            jax.ShapeDtypeStruct((2, devices, tok_dev, column_band), jnp.bfloat16),
+            jax.ShapeDtypeStruct((groups, 2, 2 * tok_dev, padded), jnp.bfloat16),
+            jax.ShapeDtypeStruct((2, padded, column_band), jnp.float32),
+        ),
+        in_specs=[hbm] * 5,
+        out_specs=(vmem,) * 3,
         scratch_shapes=[
+            pltpu.VMEM(hidden.shape, jnp.bfloat16),
+            pltpu.VMEM(attn_out.shape, jnp.bfloat16),
+            pltpu.VMEM(gain_attn.shape, jnp.bfloat16),
+            pltpu.VMEM(gain_mlp.shape, jnp.bfloat16),
+            pltpu.SMEM(lengths.shape, jnp.int32),
             pltpu.VMEM((2, 2, tok_dev, column_band), jnp.bfloat16),
-            pltpu.VMEM((2, devices, tok_dev, column_band), jnp.bfloat16),
-            pltpu.VMEM((groups, 2, 2 * tok_dev, padded), jnp.bfloat16),
-            pltpu.VMEM((2, padded, column_band), jnp.float32),
+            semaphores((5,)),
             semaphores((2, devices)),
             semaphores((groups,)),
             semaphores((groups,)),
@@ -288,9 +343,25 @@
             semaphores((2, devices)),
         ],
         compiler_params=pltpu.CompilerParams(
-            collective_id=0, has_side_effects=True, vmem_limit_bytes=48 * 2**20
+            collective_id=0, has_side_effects=True, vmem_limit_bytes=24 * 2**20
         ),
-    )(hidden, attn_out, gain_attn.reshape(1, width), gain_mlp.reshape(1, width), lengths)
+    )(*(
+        pltpu.with_memory_space_constraint(array, pltpu.HBM)
+        for array in (hidden, attn_out, gain_attn, gain_mlp, lengths)
+    ))
+    shape = (1, row_count, column_band)
+    n_bands = 2
+    return pl.pallas_call(
+        last_kernel,
+        out_shape=(jax.ShapeDtypeStruct(shape, jnp.float32),) * 2,
+        in_specs=[vmem] * 3,
+        out_specs=(hbm, hbm),
+        scratch_shapes=[
+            pltpu.VMEM((2,) + shape, jnp.float32),
+            semaphores((2, n_bands)),
+        ],
+        compiler_params=pltpu.CompilerParams(vmem_limit_bytes=12 * 2**20),
+    )(held, rows, total)
 
 
 def from_partner(block, axis, distance):

time: 55 us -> 51.1 us (0.929)
  local copies, waits for them, and re-layouts: 6.25 us -> 0 us
  Pallas kernels: 47.1 us -> 49.9 us
    unnamed x8 -> x0, local copies, waits for them, and re-layouts: 4.83 us -> none
    pallas_call x1 -> x2, Pallas kernels: 47.1 us -> 49.9 us  [the longest x1 47.9 us: gathered(): pl.pallas_call(gather_kernel, out_shape=(jax.ShapeDtypeStruct((2, devices...]
    reshape x2 -> x0, local copies, waits for them, and re-layouts: 1.42 us -> none  [the longest x1 0.71 us: gathered(): gain_mlp.reshape(1, width)]
where the time goes in v2:
time: 51.1 us; the launch traced here: 50.6 us
  Pallas kernels  49.9 us (98%)
  between operations  0.64 us (1%)
    pallas_call x1, Pallas kernels, gathered(): pl.pallas_call(gather_kernel, out_shape=(jax.ShapeDtypeStruct((2, devices...  47.9 us
    pallas_call x1, Pallas kernels, gathered(): pl.pallas_call(last_kernel, out_shape=(jax.ShapeDtypeStruct(shape, jnp.fl...  2.05 us

profile of v2, /device:TPU:0, one launch (start us, length us, event | category | flops | bytes accessed | tf_op | source)
XLA Modules:
  0.0 50.6 jit_solution(12022212042341680313)
XLA Ops:
  0.6 47.9 %shard_map.68 = (bf16[2,32,32,1792]{3,2,1,0:T(8,128)(2,1)S(1)}, bf16[16,2,64,256]{3,2,1,0:T(8,128)(2,1)S(1)}, f32[2,256,1792]{2,1,0:T(8,128)S(1)}) custom-call(bf16[1,32,3584]{2,1,0:T(8,128)(2,1)} %hidden_hbm.1, bf16[1,32,3584]{2,1,0:T(8,128)(2,1)} %attn_hbm.1, bf16[3584]{0:T(1024)(128)(2,1)} %gain_attn_hbm.1, bf16[3584]{0:T(1024)(128)(2,1)} %gain_mlp_hbm.1, ...), custom_call_target="tpu_custom_call" | custom-call | tf_op jit(solution)/shard_map/pallas_call | solution.py:321
  48.5 2.1 %shard_map.69 = (f32[1,224,1792]{2,1,0:T(8,128)}, f32[1,224,1792]{2,1,0:T(8,128)}) custom-call(bf16[2,32,32,1792]{3,2,1,0:T(8,128)(2,1)S(1)} %get-tuple-element.5.held, bf16[16,2,64,256]{3,2,1,0:T(8,128)(2,1)S(1)} %get-tuple-element.6.rows, f32[2,256,1792]{2,1,0:T(8,128)S(1)} %get-tuple-element.7.total), custom_call_target="tpu_custom_call" | custom-call | tf_op jit(solution)/shard_map/pallas_call | solution.py:354

commit v3 on v2

--- a/solution.py
+++ b/solution.py
@@ -56,7 +56,7 @@
 
 def gather_kernel(
     hidden_hbm, attn_hbm, gain_attn_hbm, gain_mlp_hbm, lengths_hbm, held, rows, total,
-    hidden, attn_out, gain_attn, gain_mlp, lengths, mine,
+    hidden, attn_out, gain_attn, gain_mlp, lengths, mine, lent,
     loaded, got, row_got, row_sent, z_sent, side_sent, pair_sent,
 ):
     task, tok = lax.axis_index("task"), lax.axis_index("tok")
@@ -208,27 +208,50 @@
             device_id_type=pl.DeviceIdType.MESH,
         )
 
-    def rows_of(step, tasks, other_arrived=True):
+    def lend_copy(tasks):
+        group = plane_1 * n_task + tasks
+        return pltpu.make_async_remote_copy(
+            src_ref=lent.at[tasks], dst_ref=rows.at[group], send_sem=row_sent.at[group],
+            recv_sem=row_got.at[group], device_id=to_3,
+            device_id_type=pl.DeviceIdType.MESH,
+        )
+
+    def rows_of(step, tasks):
         for which in range(2):
             arrive(which, chunk(order[step], tasks, 1 - core))
         group = order[step] * n_task + tasks
 
-        @pl.when(outer)
-        def _():
+        def cut_into(target):
             for which in range(2):
                 span = held[
                     which, pl.ds(group * 2, 2), :, pl.ds(pl.multiple_of(base, LANES), window)
                 ]
                 span = span.reshape(2 * tok_dev, window).astype(jnp.float32)
                 span = pltpu.roll(span, shift, 1)
-                rows[group, which] = span[:, :padded].astype(jnp.bfloat16)
-
-        return group
-
-    def send_rows(group):
+                target[which] = span[:, :padded].astype(jnp.bfloat16)
+
         @pl.when(outer)
         def _():
-            row_copy(group).start()
+            cut_into(rows.at[group])
+
+        if step == 1:
+            @pl.when(inner)
+            def _():
+                cut_into(lent.at[tasks])
+
+        return step, tasks, group
+
+    def send_rows(waiting):
+        step, tasks, group = waiting
+        if step < n_planes - 1:
+            @pl.when(outer)
+            def _():
+                row_copy(group).start()
+
+        if step == 1:
+            @pl.when(inner)
+            def _():
+                lend_copy(tasks).start()
 
     def cut(step, members):
         waiting = None
@@ -301,11 +324,14 @@
         for which in range(2):
             to_inner(which).wait_send()
             relay(which).wait_send()
+        for tasks in range(n_task):
+            lend_copy(tasks).wait_send()
 
     @pl.when(outer)
     def _():
-        for group in range(n_planes * n_task):
-            row_copy(group).wait_send()
+        for step in range(n_planes - 1):
+            for tasks in range(n_task):
+                row_copy(order[step] * n_task + tasks).wait_send()
 
 
 def gathered(hidden, attn_out, gain_attn, gain_mlp, lengths):
@@ -334,6 +360,7 @@
             pltpu.VMEM(gain_mlp.shape, jnp.bfloat16),
             pltpu.SMEM(lengths.shape, jnp.int32),
             pltpu.VMEM((2, 2, tok_dev, column_band), jnp.bfloat16),
+            pltpu.VMEM((n_task, 2, 2 * tok_dev, padded), jnp.bfloat16),
             semaphores((5,)),
             semaphores((2, devices)),
             semaphores((groups,)),

time: 51.1 us -> 46.4 us (0.908)
  the two profiles are of different devices: /device:TPU:0 before, /device:TPU:20 now
where the time goes in v3:
time: 46.4 us; the launch traced here: 46.2 us
  Pallas kernels  45.6 us (98%)
  between operations  0.64 us (1%)
    pallas_call x1, Pallas kernels, gathered(): pl.pallas_call(gather_kernel, out_shape=(jax.ShapeDtypeStruct((2, devices...  43.5 us
    pallas_call x1, Pallas kernels, gathered(): pl.pallas_call(last_kernel, out_shape=(jax.ShapeDtypeStruct(shape, jnp.fl...  2.05 us

profile of v3, /device:TPU:20, one launch (start us, length us, event | category | flops | bytes accessed | tf_op | source)
XLA Modules:
  0.0 46.2 jit_solution(17789546409622446339)
XLA Ops:
  0.6 43.5 %shard_map.68 = (bf16[2,32,32,1792]{3,2,1,0:T(8,128)(2,1)S(1)}, bf16[16,2,64,256]{3,2,1,0:T(8,128)(2,1)S(1)}, f32[2,256,1792]{2,1,0:T(8,128)S(1)}) custom-call(bf16[1,32,3584]{2,1,0:T(8,128)(2,1)} %hidden_hbm.1, bf16[1,32,3584]{2,1,0:T(8,128)(2,1)} %attn_hbm.1, bf16[3584]{0:T(1024)(128)(2,1)} %gain_attn_hbm.1, bf16[3584]{0:T(1024)(128)(2,1)} %gain_mlp_hbm.1, ...), custom_call_target="tpu_custom_call" | custom-call | tf_op jit(solution)/shard_map/pallas_call | solution.py:347
  44.2 2.1 %shard_map.69 = (f32[1,224,1792]{2,1,0:T(8,128)}, f32[1,224,1792]{2,1,0:T(8,128)}) custom-call(bf16[2,32,32,1792]{3,2,1,0:T(8,128)(2,1)S(1)} %get-tuple-element.5.held, bf16[16,2,64,256]{3,2,1,0:T(8,128)(2,1)S(1)} %get-tuple-element.6.rows, f32[2,256,1792]{2,1,0:T(8,128)S(1)} %get-tuple-element.7.total), custom_call_target="tpu_custom_call" | custom-call | tf_op jit(solution)/shard_map/pallas_call | solution.py:381

commit v4 on v3

--- a/solution.py
+++ b/solution.py
@@ -8,6 +8,7 @@
 from jax.sharding import PartitionSpec as P
 
 LANES = 128
+LENT = (2, 3)
 
 
 def planes_in_product_order():
@@ -208,15 +209,23 @@
             device_id_type=pl.DeviceIdType.MESH,
         )
 
-    def lend_copy(tasks):
-        group = plane_1 * n_task + tasks
+    everyone = (task, task_x, task_y, task_d)
+    lends = [(1, member) for member in range(4)] + [(0, member) for member in LENT]
+    gives = [
+        (step, member) for step in range(n_planes - 1) for member in range(4)
+        if step < 2 or (0, member) not in lends
+    ]
+
+    def lend_copy(step, tasks):
+        group = order[step] * n_task + tasks
         return pltpu.make_async_remote_copy(
-            src_ref=lent.at[tasks], dst_ref=rows.at[group], send_sem=row_sent.at[group],
+            src_ref=lent.at[step, tasks], dst_ref=rows.at[group], send_sem=row_sent.at[group],
             recv_sem=row_got.at[group], device_id=to_3,
             device_id_type=pl.DeviceIdType.MESH,
         )
 
-    def rows_of(step, tasks):
+    def rows_of(step, member):
+        tasks = everyone[member]
         for which in range(2):
             arrive(which, chunk(order[step], tasks, 1 - core))
         group = order[step] * n_task + tasks
@@ -234,29 +243,29 @@
         def _():
             cut_into(rows.at[group])
 
-        if step == 1:
+        if (step, member) in lends:
             @pl.when(inner)
             def _():
-                cut_into(lent.at[tasks])
-
-        return step, tasks, group
+                cut_into(lent.at[step, tasks])
+
+        return step, member, group
 
     def send_rows(waiting):
-        step, tasks, group = waiting
-        if step < n_planes - 1:
+        step, member, group = waiting
+        if (step, member) in gives:
             @pl.when(outer)
             def _():
                 row_copy(group).start()
 
-        if step == 1:
+        if (step, member) in lends:
             @pl.when(inner)
             def _():
-                lend_copy(tasks).start()
+                lend_copy(step, everyone[member]).start()
 
     def cut(step, members):
         waiting = None
-        for tasks in members:
-            group = rows_of(step, tasks)
+        for member in members:
+            group = rows_of(step, member)
             if waiting is not None:
                 send_rows(waiting)
             waiting = group
@@ -279,31 +288,30 @@
             else:
                 total[which] += piece
 
-    sides = (task, task_x, task_y)
-    everyone = sides + (task_d,)
+    every, sides = range(4), range(3)
     for which in range(2):
         own_step(0, which)
     for which in range(2):
+        side_step(0, which)
         own_step(1, which)
-        side_step(0, which)
-    for which in range(2):
+    for which in range(2):
+        side_step(1, which)
         own_step(2, which)
-        side_step(1, which)
         diagonal_step(0, which)
-    waiting = cut(0, everyone)
-    for which in range(2):
-        own_step(3, which)
+    waiting = cut(0, every)
+    for which in range(2):
+        side_step(2, which)
         if which == 0:
             send_rows(waiting)
-        side_step(2, which)
+        own_step(3, which)
         diagonal_step(1, which)
-    waiting = cut(1, everyone)
+    waiting = cut(1, every)
     for which in range(2):
         side_step(3, which)
         if which == 0:
             send_rows(waiting)
         diagonal_step(2, which)
-    waiting = cut(2, everyone)
+    waiting = cut(2, every)
     multiply(0)
     send_rows(waiting)
     waiting = cut(3, sides)
@@ -311,9 +319,8 @@
     send_rows(waiting)
     for which in range(2):
         diagonal_step(3, which)
-    waiting = cut(3, (task_d,))
     multiply(2)
-    send_rows(waiting)
+    cut(3, (3,))
     rows_arrive(3)
 
     for out in started:
@@ -324,14 +331,13 @@
         for which in range(2):
             to_inner(which).wait_send()
             relay(which).wait_send()
-        for tasks in range(n_task):
-            lend_copy(tasks).wait_send()
+        for step, member in lends:
+            lend_copy(step, everyone[member]).wait_send()
 
     @pl.when(outer)
     def _():
-        for step in range(n_planes - 1):
-            for tasks in range(n_task):
-                row_copy(order[step] * n_task + tasks).wait_send()
+        for step, member in gives:
+            row_copy(order[step] * n_task + everyone[member]).wait_send()
 
 
 def gathered(hidden, attn_out, gain_attn, gain_mlp, lengths):
@@ -360,7 +366,7 @@
             pltpu.VMEM(gain_mlp.shape, jnp.bfloat16),
             pltpu.SMEM(lengths.shape, jnp.int32),
             pltpu.VMEM((2, 2, tok_dev, column_band), jnp.bfloat16),
-            pltpu.VMEM((n_task, 2, 2 * tok_dev, padded), jnp.bfloat16),
+            pltpu.VMEM((2, n_task, 2, 2 * tok_dev, padded), jnp.bfloat16),
             semaphores((5,)),
             semaphores((2, devices)),
             semaphores((groups,)),

time: 46.4 us -> 45 us (0.970)
  the two profiles are of different devices: /device:TPU:20 before, /device:TPU:0 now
where the time goes in v4:
time: 45 us; the launch traced here: 44.9 us
  Pallas kernels  44.2 us (98%)
  between operations  0.64 us (1%)
    pallas_call x1, Pallas kernels, gathered(): pl.pallas_call(gather_kernel, out_shape=(jax.ShapeDtypeStruct((2, devices...  42.2 us
    pallas_call x1, Pallas kernels, gathered(): pl.pallas_call(last_kernel, out_shape=(jax.ShapeDtypeStruct(shape, jnp.fl...  2.05 us

profile of v4, /device:TPU:0, one launch (start us, length us, event | category | flops | bytes accessed | tf_op | source)
XLA Modules:
  0.0 44.9 jit_solution(10321120256562448768)
XLA Ops:
  0.6 42.2 %shard_map.68 = (bf16[2,32,32,1792]{3,2,1,0:T(8,128)(2,1)S(1)}, bf16[16,2,64,256]{3,2,1,0:T(8,128)(2,1)S(1)}, f32[2,256,1792]{2,1,0:T(8,128)S(1)}) custom-call(bf16[1,32,3584]{2,1,0:T(8,128)(2,1)} %hidden_hbm.1, bf16[1,32,3584]{2,1,0:T(8,128)(2,1)} %attn_hbm.1, bf16[3584]{0:T(1024)(128)(2,1)} %gain_attn_hbm.1, bf16[3584]{0:T(1024)(128)(2,1)} %gain_mlp_hbm.1, ...), custom_call_target="tpu_custom_call" | custom-call | tf_op jit(solution)/shard_map/pallas_call | solution.py:353
  42.8 2.1 %shard_map.69 = (f32[1,224,1792]{2,1,0:T(8,128)}, f32[1,224,1792]{2,1,0:T(8,128)}) custom-call(bf16[2,32,32,1792]{3,2,1,0:T(8,128)(2,1)S(1)} %get-tuple-element.5.held, bf16[16,2,64,256]{3,2,1,0:T(8,128)(2,1)S(1)} %get-tuple-element.6.rows, f32[2,256,1792]{2,1,0:T(8,128)S(1)} %get-tuple-element.7.total), custom_call_target="tpu_custom_call" | custom-call | tf_op jit(solution)/shard_map/pallas_call | solution.py:387
